TPU v7x, 256 devices: a whole 4x4x8 slice. The times are simulated.
256 devices in a mesh: gx: 8 (over y, core), gy: 32 (over z, x).
Axes of the slice: x: 4, y: 4, z: 8, core: 2. Of those that a mesh axis runs over, the one named last changes fastest.
Arguments:
- rhs_values: float32 [32, 524288], P(None, ('gx', 'gy')), may hold values from -6 to 6
- point_coords: float32 [3, 524288], P(None, ('gx', 'gy')), may hold values from 0 to 1, as said below
- leaf_basis: float32 [64, 524288], P(None, ('gx', 'gy')), may hold values from -0.375 to 0.375
- leaf_transfer: float32 [2048, 64, 64], P(('gx', 'gy')), may hold values from -0.75 to 0.75
- cluster_transfer: float32 [256, 64, 64], P(('gx', 'gy')), may hold values from -0.125 to 0.125
- near_list: int32 [2048, 12], P(('gx', 'gy')), may hold values from -1 to 2047, as said below
- coupling_list: int32 [256, 4], P(('gx', 'gy')), may hold values from -1 to 31, as said below
- coupling: float32 [256, 4, 64, 64], P(('gx', 'gy')), may hold values from -0.375 to 0.375
- top_coupling: float32 [8, 8, 64, 64], P('gx'), may hold values from -0.25 to 0.25
Outputs:
- product: float32 [32, 524288], P(None, ('gx', 'gy'))
Inputs may be any that keep to these rules, and one draw needn't show every extreme that they name: `near_list`: row t lists distinct leaves that lie within 6 positions of t, t itself first, then the other used entries, then -1 in the unused slots; some leaf uses all 12 slots. `coupling_list`: row d lists distinct positions within the group of cluster d, never the position d % 32 or the ones beside it, used entries first and -1 in the unused slots; some row uses all 4 slots. `point_coords`: the points lie on a closed surface; each leaf's points fill one patch of it, and the leaves follow a Morton order of the patches.
All inputs are finite; a program needn't handle non-finite values.
Results may differ from a plain program's by a relative error of at most 0.0003.
Values sent between devices are 32-bit elements; how exact they have to be, the bound alone decides.
A program may use at most 64 MiB of HBM per device.

v0:
```python
import jax
import jax.numpy as jnp
from jax import lax
from jax.sharding import PartitionSpec as P

LEAF = 256
NEAR = 12
REACH = 6


precise = lax.Precision.HIGHEST
wavenumber = 300.0
softening = 0.0001
core_scale = 0.03


def passed_along(array, axis, by):
    devices = lax.axis_size(axis)
    pairs = [(i, i + by) for i in range(devices) if 0 <= i + by < devices]
    return lax.ppermute(array, axis, pairs)


def joined_along(parts, dim):
    dims = list(parts.shape[1:])
    dims[dim] *= parts.shape[0]
    return jnp.moveaxis(parts, 0, dim).reshape(dims)


def from_everyone(array, axis):
    devices = lax.axis_size(axis)
    return lax.all_to_all(
        jnp.broadcast_to(array[None], (devices, *array.shape)), axis, 0, 0, tiled=True
    )


def gather_directly(array, axis, dim):
    return joined_along(from_everyone(array, axis), dim)


def taken_together(array, axis):
    return from_everyone(array, axis).sum(axis=0)


def kernel_tile(targets, sources):
    squared = jnp.zeros(targets.shape[1:2] + (sources.shape[2], targets.shape[2]), targets.dtype)
    for component in range(3):
        gap_part = sources[component][:, :, None] - targets[component][:, None, :]
        squared = squared + gap_part * gap_part
    scale_factor = core_scale * (NEAR * LEAF) ** (-0.5)
    return jnp.cos(wavenumber * jnp.sqrt(squared)) * lax.rsqrt(squared + softening) * scale_factor


def per_device(
    rhs_values,
    point_coords,
    leaf_basis,
    leaf_transfer,
    cluster_transfer,
    near_list,
    coupling_list,
    coupling,
    top_coupling,
):
    leaf_count = near_list.shape[0]
    value_rows = rhs_values.shape[0]
    device_index = lax.axis_index("gx") * lax.axis_size("gy") + lax.axis_index("gy")
    stacked = jnp.concatenate([rhs_values, point_coords], axis=0)
    edge_cols = REACH * LEAF
    below_rim = passed_along(stacked[:, -edge_cols:], ("gx", "gy"), 1)
    above_rim = passed_along(stacked[:, :edge_cols], ("gx", "gy"), -1)
    table_base = device_index * leaf_count - REACH
    source_table = jnp.concatenate([below_rim, stacked, above_rim], axis=1)
    source_table = source_table.reshape(value_rows + 3, source_table.shape[1] // LEAF, LEAF)
    source_vals_all = source_table[:value_rows]
    source_pts_all = source_table[value_rows:]
    targets = point_coords.reshape(3, leaf_count, LEAF)
    usable_all = near_list >= 0
    clipped_all = jnp.where(usable_all, near_list - table_base, 0)

    def add_slot(slot_index, running):
        column = lax.dynamic_index_in_dim(clipped_all, slot_index, 1, keepdims=False)
        usable = lax.dynamic_index_in_dim(usable_all, slot_index, 1, keepdims=False)
        source_vals = jnp.where(
            usable[None, :, None], jnp.take(source_vals_all, column, axis=1), 0.0
        )
        source_pts = jnp.take(source_pts_all, column, axis=1)
        tile = kernel_tile(targets, source_pts)
        return running + jnp.einsum("rlj,lji->rli", source_vals, tile, precision=precise)

    start = jnp.zeros((value_rows, leaf_count, LEAF), jnp.float32)
    near_values = lax.fori_loop(0, NEAR, add_slot, start)
    leaf_values = rhs_values.reshape(value_rows, leaf_count, LEAF)
    leaf_bases = leaf_basis.reshape(leaf_basis.shape[0], leaf_count, LEAF)
    leaf_coeffs = jnp.einsum("rlj,klj->lrk", leaf_values, leaf_bases, precision=precise)
    cluster_coeffs = jnp.einsum("lrk,lkm->rm", leaf_coeffs, leaf_transfer, precision=precise)
    group_coeff_table = gather_directly(cluster_coeffs[None], "gy", 0)
    partner_ids = coupling_list[0]
    positions = jnp.arange(group_coeff_table.shape[0], dtype=jnp.int32)
    onehot = jnp.where(partner_ids[:, None] == positions[None, :], 1.0, 0.0).astype(jnp.float32)
    selected = jnp.einsum("kq,qrm->krm", onehot, group_coeff_table, precision=precise)
    coupled = jnp.einsum("krm,kmn->rn", selected, coupling[0], precision=precise)
    cluster_terms = jnp.dot(cluster_coeffs, cluster_transfer[0], precision=precise)
    group_sums = taken_together(cluster_terms, "gy")
    all_groups = gather_directly(group_sums[None], "gx", 0)
    group_here = lax.axis_index("gx")
    group_ids = jnp.arange(all_groups.shape[0], dtype=jnp.int32)
    far_mask = jnp.where(jnp.abs(group_ids - group_here) >= 2, 1.0, 0.0).astype(jnp.float32)
    top_field = jnp.einsum(
        "h,hrk,hkm->rm", far_mask, all_groups, top_coupling[0], precision=precise
    )
    cluster_field = coupled + jnp.einsum(
        "rm,km->rk", top_field, cluster_transfer[0], precision=precise
    )
    leaf_field = jnp.einsum("rm,lkm->lrk", cluster_field, leaf_transfer, precision=precise)
    far_values = jnp.einsum("lrk,klj->rlj", leaf_field, leaf_bases, precision=precise)
    return (near_values + far_values).reshape(value_rows, leaf_count * LEAF)


def solution(mesh):
    return jax.shard_map(
        per_device,
        mesh=mesh,
        in_specs=(
            P(None, ("gx", "gy")),
            P(None, ("gx", "gy")),
            P(None, ("gx", "gy")),
            P(("gx", "gy"), None, None),
            P(("gx", "gy"), None, None),
            P(("gx", "gy"), None),
            P(("gx", "gy"), None),
            P(("gx", "gy"), None, None, None),
            P("gx", None, None, None),
        ),
        out_specs=P(None, ("gx", "gy")),
        check_vma=False,
    )
```

profile of v0, /device:TPU:1, one launch (start us, length us, event | category | flops | bytes accessed | tf_op | source)
XLA Modules:
  0.0 209.4 jit_solution(11478295058357939170)
XLA Ops:
  0.0 1.0 constant_dynamic-update-slice_fusion.1
  1.0 0.8 constant_dynamic-update-slice_fusion
  1.9 11.1 %collective-permute-start.1 = (f32[35,1536]{1,0:T(8,128)S(1)}, f32[35,1536]{1,0:T(8,128)S(1)}, u32[]{:S(2)}, u32[]{:S(2)}) collective-permute-start(f32[35,1536]{1,0:T(8,128)S(1)} %get-tuple-element.208), channel_id=1, source_target_pairs={{1,0},{2,1},{3,2},{4,3},{5,4},{6,5},{7,6},{8,7},{9,8},{10,9},{11,1... | collective-permute-start | bytes 645128 | tf_op jit(solution)/shard_map/ppermute | solution.py:20
  13.0 1.9 collective-permute-start
  15.9 1.0 reshape.75
  16.9 7.1 %all-to-all-start = ((f32[32,1,2048]{2,1,0:T(1,128)}), f32[32,1,2048]{2,1,0:T(1,128)S(1)}, u32[]{:S(2)}, u32[]{:S(2)}) async-start(f32[32,1,2048]{2,1,0:T(1,128)} %reshape.75), calls=%async_computation | async-start | bytes 524288 | tf_op jit(solution)/shard_map/all_to_all | solution.py:31
  24.4 1.0 reshape.77
  25.4 1.0 collective-permute-done
  26.6 9.1 %all-to-all-done = f32[32,1,2048]{2,1,0:T(1,128)S(1)} async-done(((f32[32,1,2048]{2,1,0:T(1,128)}), f32[32,1,2048]{2,1,0:T(1,128)S(1)}, u32[]{:S(2)}, u32[]{:S(2)}) %all-to-all-start) | async-done | bytes 262176 | tf_op jit(solution)/shard_map/all_to_all | solution.py:31
  35.6 4.5 %all-to-all-start.1 = ((f32[32,1,2048]{2,1,0:T(1,128)}), f32[32,1,2048]{2,1,0:T(1,128)S(1)}, u32[]{:S(2)}, u32[]{:S(2)}) async-start(f32[32,1,2048]{2,1,0:T(1,128)} %reshape.77), calls=%async_computation.1 | async-start | bytes 524288 | tf_op jit(solution)/shard_map/all_to_all | solution.py:31
  40.2 150.2 %while.14 = (s32[]{:T(128)}, f32[32,8,256]{2,0,1:T(8,128)S(1)}, s32[8,12]{0,1:T(8,128)S(1)}, f32[3,20,256]{2,0,1:T(4,128)S(1)}, f32[3,8,256]{2,1,0:T(8,128)S(1)}...) while((s32[]{:T(128)}, f32[32,8,256]{2,0,1:T(8,128)S(1)}, ...), condition=%wide.region_1.2_spmd.clone, body=%wide.region_0.1_spmd.clone.sunk | while | flops 207887408 | bytes 1610055 | solution.py:91
  41.5 11.2 %fusion.86 = f32[32,8,256]{2,0,1:T(8,128)S(1)} fusion(f32[8,256]{1,0:T(8,128)S(1)} %get-tuple-element.266, f32[8,256]{1,0:T(8,128)S(1)} %get-tuple-element.269, f32[8,256]{1,0:T(8,128)S(1)} %get-tuple-element.270, f32[8,256]{1,0:T(8,128)S(1)} %get-tuple-element.271, f32[8,256]{1,0:T(8,128)S(1)} %get-tuple-element.272, ...), kind=kOutput, calls=%fused_computation.19.clone.1 | convolution fusion | flops 207880192 | bytes 835601 | tf_op jit(solution)/shard_map/while/body/eval_jaxpr/rlj,lji->rli/dot_general | solution.py:88
  54.1 11.2 %fusion.86 = f32[32,8,256]{2,0,1:T(8,128)S(1)} fusion(f32[8,256]{1,0:T(8,128)S(1)} %get-tuple-element.266, f32[8,256]{1,0:T(8,128)S(1)} %get-tuple-element.269, f32[8,256]{1,0:T(8,128)S(1)} %get-tuple-element.270, f32[8,256]{1,0:T(8,128)S(1)} %get-tuple-element.271, f32[8,256]{1,0:T(8,128)S(1)} %get-tuple-element.272, ...), kind=kOutput, calls=%fused_computation.19.clone.1 | convolution fusion | flops 207880192 | bytes 835601 | tf_op jit(solution)/shard_map/while/body/eval_jaxpr/rlj,lji->rli/dot_general | solution.py:88
  66.6 11.2 %fusion.86 = f32[32,8,256]{2,0,1:T(8,128)S(1)} fusion(f32[8,256]{1,0:T(8,128)S(1)} %get-tuple-element.266, f32[8,256]{1,0:T(8,128)S(1)} %get-tuple-element.269, f32[8,256]{1,0:T(8,128)S(1)} %get-tuple-element.270, f32[8,256]{1,0:T(8,128)S(1)} %get-tuple-element.271, f32[8,256]{1,0:T(8,128)S(1)} %get-tuple-element.272, ...), kind=kOutput, calls=%fused_computation.19.clone.1 | convolution fusion | flops 207880192 | bytes 835601 | tf_op jit(solution)/shard_map/while/body/eval_jaxpr/rlj,lji->rli/dot_general | solution.py:88
  79.1 11.2 %fusion.86 = f32[32,8,256]{2,0,1:T(8,128)S(1)} fusion(f32[8,256]{1,0:T(8,128)S(1)} %get-tuple-element.266, f32[8,256]{1,0:T(8,128)S(1)} %get-tuple-element.269, f32[8,256]{1,0:T(8,128)S(1)} %get-tuple-element.270, f32[8,256]{1,0:T(8,128)S(1)} %get-tuple-element.271, f32[8,256]{1,0:T(8,128)S(1)} %get-tuple-element.272, ...), kind=kOutput, calls=%fused_computation.19.clone.1 | convolution fusion | flops 207880192 | bytes 835601 | tf_op jit(solution)/shard_map/while/body/eval_jaxpr/rlj,lji->rli/dot_general | solution.py:88
  91.6 11.2 %fusion.86 = f32[32,8,256]{2,0,1:T(8,128)S(1)} fusion(f32[8,256]{1,0:T(8,128)S(1)} %get-tuple-element.266, f32[8,256]{1,0:T(8,128)S(1)} %get-tuple-element.269, f32[8,256]{1,0:T(8,128)S(1)} %get-tuple-element.270, f32[8,256]{1,0:T(8,128)S(1)} %get-tuple-element.271, f32[8,256]{1,0:T(8,128)S(1)} %get-tuple-element.272, ...), kind=kOutput, calls=%fused_computation.19.clone.1 | convolution fusion | flops 207880192 | bytes 835601 | tf_op jit(solution)/shard_map/while/body/eval_jaxpr/rlj,lji->rli/dot_general | solution.py:88
  104.1 11.2 %fusion.86 = f32[32,8,256]{2,0,1:T(8,128)S(1)} fusion(f32[8,256]{1,0:T(8,128)S(1)} %get-tuple-element.266, f32[8,256]{1,0:T(8,128)S(1)} %get-tuple-element.269, f32[8,256]{1,0:T(8,128)S(1)} %get-tuple-element.270, f32[8,256]{1,0:T(8,128)S(1)} %get-tuple-element.271, f32[8,256]{1,0:T(8,128)S(1)} %get-tuple-element.272, ...), kind=kOutput, calls=%fused_computation.19.clone.1 | convolution fusion | flops 207880192 | bytes 835601 | tf_op jit(solution)/shard_map/while/body/eval_jaxpr/rlj,lji->rli/dot_general | solution.py:88
  116.6 11.2 %fusion.86 = f32[32,8,256]{2,0,1:T(8,128)S(1)} fusion(f32[8,256]{1,0:T(8,128)S(1)} %get-tuple-element.266, f32[8,256]{1,0:T(8,128)S(1)} %get-tuple-element.269, f32[8,256]{1,0:T(8,128)S(1)} %get-tuple-element.270, f32[8,256]{1,0:T(8,128)S(1)} %get-tuple-element.271, f32[8,256]{1,0:T(8,128)S(1)} %get-tuple-element.272, ...), kind=kOutput, calls=%fused_computation.19.clone.1 | convolution fusion | flops 207880192 | bytes 835601 | tf_op jit(solution)/shard_map/while/body/eval_jaxpr/rlj,lji->rli/dot_general | solution.py:88
  129.2 11.2 %fusion.86 = f32[32,8,256]{2,0,1:T(8,128)S(1)} fusion(f32[8,256]{1,0:T(8,128)S(1)} %get-tuple-element.266, f32[8,256]{1,0:T(8,128)S(1)} %get-tuple-element.269, f32[8,256]{1,0:T(8,128)S(1)} %get-tuple-element.270, f32[8,256]{1,0:T(8,128)S(1)} %get-tuple-element.271, f32[8,256]{1,0:T(8,128)S(1)} %get-tuple-element.272, ...), kind=kOutput, calls=%fused_computation.19.clone.1 | convolution fusion | flops 207880192 | bytes 835601 | tf_op jit(solution)/shard_map/while/body/eval_jaxpr/rlj,lji->rli/dot_general | solution.py:88
  141.7 11.2 %fusion.86 = f32[32,8,256]{2,0,1:T(8,128)S(1)} fusion(f32[8,256]{1,0:T(8,128)S(1)} %get-tuple-element.266, f32[8,256]{1,0:T(8,128)S(1)} %get-tuple-element.269, f32[8,256]{1,0:T(8,128)S(1)} %get-tuple-element.270, f32[8,256]{1,0:T(8,128)S(1)} %get-tuple-element.271, f32[8,256]{1,0:T(8,128)S(1)} %get-tuple-element.272, ...), kind=kOutput, calls=%fused_computation.19.clone.1 | convolution fusion | flops 207880192 | bytes 835601 | tf_op jit(solution)/shard_map/while/body/eval_jaxpr/rlj,lji->rli/dot_general | solution.py:88
  154.2 11.2 %fusion.86 = f32[32,8,256]{2,0,1:T(8,128)S(1)} fusion(f32[8,256]{1,0:T(8,128)S(1)} %get-tuple-element.266, f32[8,256]{1,0:T(8,128)S(1)} %get-tuple-element.269, f32[8,256]{1,0:T(8,128)S(1)} %get-tuple-element.270, f32[8,256]{1,0:T(8,128)S(1)} %get-tuple-element.271, f32[8,256]{1,0:T(8,128)S(1)} %get-tuple-element.272, ...), kind=kOutput, calls=%fused_computation.19.clone.1 | convolution fusion | flops 207880192 | bytes 835601 | tf_op jit(solution)/shard_map/while/body/eval_jaxpr/rlj,lji->rli/dot_general | solution.py:88
  166.7 11.2 %fusion.86 = f32[32,8,256]{2,0,1:T(8,128)S(1)} fusion(f32[8,256]{1,0:T(8,128)S(1)} %get-tuple-element.266, f32[8,256]{1,0:T(8,128)S(1)} %get-tuple-element.269, f32[8,256]{1,0:T(8,128)S(1)} %get-tuple-element.270, f32[8,256]{1,0:T(8,128)S(1)} %get-tuple-element.271, f32[8,256]{1,0:T(8,128)S(1)} %get-tuple-element.272, ...), kind=kOutput, calls=%fused_computation.19.clone.1 | convolution fusion | flops 207880192 | bytes 835601 | tf_op jit(solution)/shard_map/while/body/eval_jaxpr/rlj,lji->rli/dot_general | solution.py:88
  179.2 11.2 %fusion.86 = f32[32,8,256]{2,0,1:T(8,128)S(1)} fusion(f32[8,256]{1,0:T(8,128)S(1)} %get-tuple-element.266, f32[8,256]{1,0:T(8,128)S(1)} %get-tuple-element.269, f32[8,256]{1,0:T(8,128)S(1)} %get-tuple-element.270, f32[8,256]{1,0:T(8,128)S(1)} %get-tuple-element.271, f32[8,256]{1,0:T(8,128)S(1)} %get-tuple-element.272, ...), kind=kOutput, calls=%fused_computation.19.clone.1 | convolution fusion | flops 207880192 | bytes 835601 | tf_op jit(solution)/shard_map/while/body/eval_jaxpr/rlj,lji->rli/dot_general | solution.py:88
  191.0 1.3 reduce
  192.5 1.3 reduce.1
  194.1 0.8 reshape.79
  194.9 6.3 %all-to-all-start.2 = ((f32[8,1,2048]{2,1,0:T(1,128)}), f32[8,1,2048]{2,1,0:T(1,128)S(1)}, u32[]{:S(2)}, u32[]{:S(2)}) async-start(f32[8,1,2048]{2,1,0:T(1,128)} %reshape.79), calls=%async_computation.2 | async-start | bytes 131072 | tf_op jit(solution)/shard_map/all_to_all | solution.py:31
  201.2 0.6 fusion.49
  202.1 4.0 %all-to-all-done.2 = f32[8,1,2048]{2,1,0:T(1,128)S(1)} async-done(((f32[8,1,2048]{2,1,0:T(1,128)}), f32[8,1,2048]{2,1,0:T(1,128)S(1)}, u32[]{:S(2)}, u32[]{:S(2)}) %all-to-all-start.2) | async-done | bytes 65568 | tf_op jit(solution)/shard_map/all_to_all | solution.py:31
  206.0 0.8 reduce.2
  207.5 0.8 convolution_bitcast_fusion.1
  208.7 0.7 copy.51
  (153 shorter events, 19.1 us)
Async XLA Ops:
  0.0 15.5 %copy-start = (f32[8,64,64]{2,1,0:T(8,128)S(1)}, f32[8,64,64]{2,1,0:T(8,128)}, u32[]{:S(2)}) copy-start(f32[8,64,64]{2,1,0:T(8,128)} %param.14) | copy-start | bytes 393220
  1.0 13.9 %copy-start.1 = (f32[64,2048]{1,0:T(8,128)S(1)}, f32[64,2048]{1,0:T(8,128)}, u32[]{:S(2)}) copy-start(f32[64,2048]{1,0:T(8,128)} %param.13) | copy-start | bytes 1572868
  1.0 13.9 %copy-start.2 = (f32[32,2048]{1,0:T(8,128)S(1)}, f32[32,2048]{1,0:T(8,128)}, u32[]{:S(2)}) copy-start(f32[32,2048]{1,0:T(8,128)} %param.11) | copy-start | bytes 786436
  1.9 23.5 %collective-permute-start.1 = (f32[35,1536]{1,0:T(8,128)S(1)}, f32[35,1536]{1,0:T(8,128)S(1)}, u32[]{:S(2)}, u32[]{:S(2)}) collective-permute-start(f32[35,1536]{1,0:T(8,128)S(1)} %get-tuple-element.208), channel_id=1, source_target_pairs={{1,0},{2,1},{3,2},{4,3},{5,4},{6,5},{7,6},{8,7},{9,8},{10,9},{11,1... | collective-permute-start | bytes 645128 | tf_op jit(solution)/shard_map/ppermute | solution.py:20
  13.0 13.4 %collective-permute-start = (f32[35,1536]{1,0:T(8,128)S(1)}, f32[35,1536]{1,0:T(8,128)S(1)}, u32[]{:S(2)}, u32[]{:S(2)}) collective-permute-start(f32[35,1536]{1,0:T(8,128)S(1)} %get-tuple-element.207), channel_id=1, source_target_pairs={{0,1},{1,2},{2,3},{3,4},{4,5},{5,6},{6,7},{7,8},{8,9},{9,10},{10,1... | collective-permute-start | bytes 645128 | tf_op jit(solution)/shard_map/ppermute | solution.py:20
  15.9 8.1 %copy-start.7 = (s32[8,12]{1,0:T(8,128)S(1)}, s32[8,12]{1,0:T(8,128)}, u32[]{:S(2)}) copy-start(s32[8,12]{1,0:T(8,128)} %param.16) | copy-start | bytes 1156
  15.9 8.2 %copy-start.4 = (f32[3,2048]{1,0:T(4,128)S(1)}, f32[3,2048]{1,0:T(4,128)}, u32[]{:S(2)}) copy-start(f32[3,2048]{1,0:T(4,128)} %param.12) | copy-start | bytes 73732
  15.9 8.2 %copy-start.5 = (f32[1,64,64]{2,1,0:T(8,128)S(1)}, f32[1,64,64]{2,1,0:T(8,128)}, u32[]{:S(2)}) copy-start(f32[1,64,64]{2,1,0:T(8,128)} %param.15) | copy-start | bytes 49156
  16.9 18.7 %all-to-all-start = ((f32[32,1,2048]{2,1,0:T(1,128)}), f32[32,1,2048]{2,1,0:T(1,128)S(1)}, u32[]{:S(2)}, u32[]{:S(2)}) async-start(f32[32,1,2048]{2,1,0:T(1,128)} %reshape.75), calls=%async_computation | async-start | bytes 524288 | tf_op jit(solution)/shard_map/all_to_all | solution.py:31
  35.6 156.9 %all-to-all-start.1 = ((f32[32,1,2048]{2,1,0:T(1,128)}), f32[32,1,2048]{2,1,0:T(1,128)S(1)}, u32[]{:S(2)}, u32[]{:S(2)}) async-start(f32[32,1,2048]{2,1,0:T(1,128)} %reshape.77), calls=%async_computation.1 | async-start | bytes 524288 | tf_op jit(solution)/shard_map/all_to_all | solution.py:31
  194.0 7.1 %copy-start.8 = (s32[1,4]{1,0:T(1,128)S(1)}, s32[1,4]{1,0:T(1,128)}, u32[]{:S(2)}) copy-start(s32[1,4]{1,0:T(1,128)} %param.17) | copy-start | bytes 52
  194.1 7.7 %copy-start.6 = (f32[1,4,64,64]{3,2,1,0:T(8,128)S(1)}, f32[1,4,64,64]{3,2,1,0:T(8,128)}, u32[]{:S(2)}) copy-start(f32[1,4,64,64]{3,2,1,0:T(8,128)} %param.18) | copy-start | bytes 196612
  194.9 12.0 %copy-start.3 = (f32[1,8,64,64]{3,2,1,0:T(8,128)S(1)}, f32[1,8,64,64]{3,2,1,0:T(8,128)}, u32[]{:S(2)}) copy-start(f32[1,8,64,64]{3,2,1,0:T(8,128)} %param.19) | copy-start | bytes 393220
  194.9 11.1 %all-to-all-start.2 = ((f32[8,1,2048]{2,1,0:T(1,128)}), f32[8,1,2048]{2,1,0:T(1,128)S(1)}, u32[]{:S(2)}, u32[]{:S(2)}) async-start(f32[8,1,2048]{2,1,0:T(1,128)} %reshape.79), calls=%async_computation.2 | async-start | bytes 131072 | tf_op jit(solution)/shard_map/all_to_all | solution.py:31
where the time goes:
time: 210 us; the launch traced here: 209 us
  matrix products  137 us (65%)
  starting transfers between devices  30.9 us (15%)
  local copies, waits for them, and re-layouts  21.1 us (10%)
  waiting for transfers between devices  14 us (7%)
  other arithmetic  4.69 us (2%)
    dot_general x12, matrix products, add_slot(): jnp.einsum('rlj,lji->rli', source_vals, tile, precision=precise)  134 us
    all_to_all x3, starting transfers between devices, from_everyone(): lax.all_to_all(jnp.broadcast_to(array[None], (devices, *array.shape)), ax...  17.9 us
    all_to_all x3, waiting for transfers between devices, from_everyone(): lax.all_to_all(jnp.broadcast_to(array[None], (devices, *array.shape)), ax...  13 us
    ppermute x2, starting transfers between devices, passed_along(): return lax.ppermute(array, axis, pairs)  13 us
    gather x12, local copies, waits for them, and re-layouts, add_slot(): source_pts = jnp.take(source_pts_all, column, axis=1)  6.92 us
    gather x12, local copies, waits for them, and re-layouts, add_slot(): jnp.take(source_vals_all, column, axis=1)  6.78 us
    unnamed x27, local copies, waits for them, and re-layouts  4.48 us
  transfers between devices with their start and end apart: 5, of which 3 were waited for; matrix products, arithmetic and copies ran while one was open for 74% of the time, Pallas kernels for 0%

commit v1 on v0

v1 whole, which is shorter than its diff:
```python
import functools

import jax
import jax.numpy as jnp
from jax import lax
from jax.experimental import pallas as pl
from jax.experimental.pallas import tpu as pltpu
from jax.sharding import PartitionSpec as P

LEAF = 256
NEAR = 12
REACH = 6
OWN = 8
RHS = 32
RANK = 64
GX = 8
GY = 32
GX_X = 4
GY_Z = 8
TABLE = OWN + REACH
FEAT = 96

F32 = jnp.float32
BF16 = jnp.bfloat16
MESH = pl.DeviceIdType.MESH

TURNS = 300.0 / 6.283185307179586
SOFT = 0.0001 * TURNS * TURNS
C2 = -4.602192823044954
C1 = 9.35955760389501
C0 = -5.69072499925369
D0 = 1.6406295037196048
COS_SCALE = 0.6095221363097632
OUT_SCALE = COS_SCALE * TURNS * 0.03 * (NEAR * LEAF) ** (-0.5)
TINY = 1e-30

FIRST = 22
CROSS = 21
TILES = 56
X_STEP = 7
Z_STEP = 19


def halves(value):
    high = value.astype(BF16)
    low = (value - high.astype(F32)).astype(BF16)
    return high, low


def thirds(value):
    high = value.astype(BF16).astype(F32)
    rest = value - high
    middle = rest.astype(BF16).astype(F32)
    low = (rest - middle).astype(BF16).astype(F32)
    return high, middle, low


def mm(left, right):
    return lax.dot_general(left, right, (((1,), (0,)), ((), ())), preferred_element_type=F32)


def mt(left, right):
    return lax.dot_general(left, right, (((1,), (1,)), ((), ())), preferred_element_type=F32)


def product(left, right, dot):
    left_high, left_low = left
    right_high, right_low = right
    return dot(left_high, right_high) + (dot(left_low, right_high) + dot(left_high, right_low))


def step_at(position, threshold):
    return lax.div(position - threshold + 64, 64)


def pair_of(position):
    position = jnp.minimum(jnp.maximum(position, 0), TILES - 1)
    past_self = step_at(position, OWN)
    past_first = step_at(position, FIRST)
    past_cross = step_at(position, FIRST + CROSS)
    crossing = past_first - past_cross
    other = past_self - crossing
    queue = lax.max(position - OWN - CROSS * past_cross + 4, 0)
    lag = 4 - lax.div(queue, 8)
    own_a = lax.rem(queue, 8)
    own_b = lax.rem(own_a + lag, 8)
    count = position - FIRST
    halo = step_at(count, 6) + step_at(count, 11) + step_at(count, 15) + step_at(count, 18) + step_at(count, 20)
    cross_a = count - lax.div(13 * halo - halo * halo, 2) + halo + 2
    cross_b = OWN + halo
    at_self = 1 - past_self
    a = at_self * position + other * own_a + crossing * cross_a
    b = at_self * position + other * own_b + crossing * cross_b
    return a, b, at_self


def kernel(
    rhs_ref,
    pts_ref,
    basis_ref,
    lt_ref,
    ct_ref,
    near_ref,
    clist_ref,
    coup_ref,
    top_ref,
    out_ref,
    xy_ref,
    centre_ref,
    left_ref,
    vals_ref,
    acc_ref,
    mask_ref,
    base_hi,
    base_lo,
    sq_a,
    sq_b,
    hi_a,
    lo_a,
    hi_b,
    lo_b,
    halo_vals,
    halo_pts,
    halo_list,
    ret_ref,
    x_ref,
    zd_ref,
    zc_ref,
    g_ref,
    halo_send,
    halo_recv,
    meta_send,
    meta_recv,
    ret_send,
    ret_recv,
    x_send,
    x_recv,
    zd_send,
    zd_recv,
    zc_send,
    zc_recv,
    g_send,
    g_recv,
):
    gx = lax.axis_index("gx")
    gy = lax.axis_index("gy")
    x_pos = lax.rem(gy, GX_X)
    z_pos = lax.div(gy, GX_X)
    wrap_up = lax.div(gy + 1, GY)
    wrap_down = lax.div(GY - gy, GY)
    following = (lax.rem(gx + wrap_up, GX), lax.rem(gy + 1, GY))
    previous = (lax.rem(gx + GX - wrap_down, GX), lax.rem(gy + GY - 1, GY))
    x_peers = [(gx, z_pos * GX_X + lax.rem(x_pos + i, GX_X)) for i in range(1, GX_X)]
    z_peers = [(gx, lax.rem(z_pos + i, GY_Z) * GX_X + x_pos) for i in range(1, GY_Z)]
    g_peers = [(lax.rem(gx + i, GX), gy) for i in range(1, GX)]

    def remote(src, dst, send, recv, device):
        return pltpu.make_async_remote_copy(
            src_ref=src, dst_ref=dst, send_sem=send, recv_sem=recv, device_id=device, device_id_type=MESH
        )

    barrier = pltpu.get_barrier_semaphore()
    greeted = [following, previous] + x_peers + z_peers + g_peers
    for device in greeted:
        pl.semaphore_signal(barrier, inc=1, device_id=device, device_id_type=MESH)

    pts_copy = remote(
        pts_ref.at[:, pl.ds(0, REACH * LEAF)], halo_pts, meta_send.at[0], meta_recv.at[0], previous
    )
    list_copy = remote(near_ref, halo_list, meta_send.at[1], meta_recv.at[1], previous)
    halo_copies = [
        remote(
            rhs_ref.at[:, pl.ds(m * LEAF, LEAF)], halo_vals.at[m], halo_send.at[m], halo_recv.at[m], previous
        )
        for m in range(REACH)
    ]
    ret_copies = [
        remote(acc_ref.at[OWN + m], ret_ref.at[m], ret_send.at[m], ret_recv.at[m], following)
        for m in range(REACH)
    ]
    x_copies = [
        remote(x_ref.at[0], x_ref.at[i], x_send.at[i - 1], x_recv.at[i - 1], x_peers[i - 1])
        for i in range(1, GX_X)
    ]
    zd_copies = [
        remote(zd_ref.at[0], zd_ref.at[i], zd_send.at[i - 1], zd_recv.at[i - 1], z_peers[i - 1])
        for i in range(1, GY_Z)
    ]
    zc_copies = [
        remote(zc_ref.at[0], zc_ref.at[i], zc_send.at[i - 1], zc_recv.at[i - 1], z_peers[i - 1])
        for i in range(1, GY_Z)
    ]
    g_copies = [
        remote(g_ref.at[0], g_ref.at[i], g_send.at[i - 1], g_recv.at[i - 1], g_peers[i - 1])
        for i in range(1, GX)
    ]

    first_leaf = (gx * GY + gy) * OWN

    def masks_from(list_value, first):
        rows = first + lax.broadcasted_iota(jnp.int32, (OWN, NEAR), 0)
        used = list_value >= 0
        found = []
        for offset in range(-REACH, REACH + 1):
            hit = jnp.where(used & (list_value == rows + offset), 1.0, 0.0)
            found.append(jnp.broadcast_to(jnp.sum(hit, axis=1, keepdims=True), (OWN, LEAF)))
        return found

    def store_values(slot, value):
        high, low = halves(value)
        vals_ref[slot, 0:RHS, :] = high
        vals_ref[slot, RHS : 2 * RHS, :] = low

    pl.semaphore_wait(barrier, len(greeted))
    pts_copy.start()
    list_copy.start()
    for copy in halo_copies:
        copy.start()

    for t in range(OWN):
        store_values(t, rhs_ref[:, t * LEAF : (t + 1) * LEAF])
    high, low = halves(basis_ref[...])
    base_hi[...] = high
    base_lo[...] = low
    own_coeffs = jnp.zeros((RHS, RANK), F32)
    for t in range(OWN):
        cols = slice(t * LEAF, (t + 1) * LEAF)
        both = mt(vals_ref[t], base_hi[:, cols])
        leaf_coeffs = both[0:RHS] + both[RHS:] + mt(vals_ref[t, 0:RHS, :], base_lo[:, cols])
        own_coeffs = own_coeffs + product(halves(leaf_coeffs), halves(lt_ref[t]), mm)
    own_terms = product(halves(own_coeffs), halves(ct_ref[0]), mm)
    x_ref[0, :, 0:RANK] = own_coeffs
    x_ref[0, :, RANK : 2 * RANK] = own_terms
    for copy in x_copies:
        copy.start()

    xy_ref[...] = jnp.zeros_like(xy_ref)
    for t in range(OWN):
        xy_ref[t, 0:3, :] = pts_ref[:, t * LEAF : (t + 1) * LEAF]
    acc_ref[...] = jnp.zeros_like(acc_ref)
    hi_b[...] = jnp.zeros_like(hi_b)
    lo_b[...] = jnp.zeros_like(lo_b)
    for index, found in enumerate(masks_from(near_ref[...], first_leaf)):
        mask_ref[index, 0:OWN, :] = found
    mask_ref[2 * REACH + 1] = jnp.zeros((2 * OWN, LEAF), F32)
    ones = jnp.ones((8, LEAF), F32)
    for t in range(OWN):
        points = xy_ref[t]
        centre = jnp.broadcast_to(jnp.sum(points, axis=1, keepdims=True) * (1.0 / LEAF), (8, LEAF))
        centre_ref[t] = centre
        high, middle, low = thirds((points - centre) * TURNS)
        whole = (points - centre) * TURNS
        sq_high, sq_middle, sq_low = thirds(whole * whole)
        high, middle, low = -2.0 * high, -2.0 * middle, -2.0 * low
        rows = jnp.concatenate(
            [high, high, middle, middle, high, low, ones, ones, ones, sq_high, sq_middle, sq_low,
             jnp.zeros((128 - FEAT, LEAF), F32)],
            axis=0,
        )
        left_ref[t] = rows.T.astype(BF16)

    def features(a, b):
        whole = (xy_ref[b] - centre_ref[a]) * TURNS
        high, middle, low = thirds(whole)
        sq_high, sq_middle, sq_low = thirds(whole * whole)
        return jnp.concatenate(
            [high, middle, high, middle, low, high, sq_high, sq_middle, sq_low, ones, ones, ones], axis=0
        ).astype(BF16)

    def squares(a, b, into):
        right = features(a, b)
        into[...] = mm(left_ref[a, :, 0:FEAT], right)

    def tile(source, into_hi, into_lo):
        for part in range(4):
            rows = slice(part * 64, part * 64 + 64)
            square = source[rows, :]
            safe = jnp.maximum(square, TINY)
            turns = safe * lax.rsqrt(safe)
            turns = turns - jnp.round(turns)
            q = turns * turns
            cubic = ((q + C2) * q + C1) * q + C0
            wave = D0 - q * (cubic * cubic)
            value = wave * lax.rsqrt(safe + SOFT)
            high = value.astype(BF16)
            into_hi[rows, :] = high
            into_lo[rows, :] = (value - high.astype(F32)).astype(BF16)

    def uses(a, b, at_self, from_hi, from_lo):
        high, low = from_hi[...], from_lo[...]
        offset = b - a
        mask_b = mask_ref[REACH - offset + (REACH + 1 + offset) * at_self, pl.ds(b, 1), :]
        mask_a = mask_ref[REACH + offset, pl.ds(a, 1), :]
        vals_a = vals_ref[a]
        vals_b = vals_ref[b]
        both = mm(vals_a, high)
        sums = both[0:RHS] + both[RHS:] + mm(vals_a[0:RHS], low)
        acc_ref[b] = acc_ref[b] + sums * mask_b
        both = mt(vals_b, high)
        sums = both[0:RHS] + both[RHS:] + mt(vals_b[0:RHS], low)
        acc_ref[a] = acc_ref[a] + sums * mask_a

    def take_meta():
        pts_copy.wait_recv()
        list_copy.wait_recv()
        for m in range(REACH):
            xy_ref[OWN + m, 0:3, :] = halo_pts[:, m * LEAF : (m + 1) * LEAF]
        for index, found in enumerate(masks_from(halo_list[...], first_leaf + OWN)):
            mask_ref[index, OWN : 2 * OWN, :] = found

    def take_values(m):
        halo_copies[m].wait_recv()
        store_values(OWN + m, halo_vals[m])

    def after_x():
        for copy in x_copies:
            copy.wait_recv()
        terms = (x_ref[0] + x_ref[1]) + (x_ref[2] + x_ref[3])
        zd_ref[0] = terms[:, RANK : 2 * RANK]
        for copy in zd_copies:
            copy.start()
        for pair in range(2):
            zc_ref[0, pair] = jnp.concatenate(
                [x_ref[2 * pair, :, 0:RANK], x_ref[2 * pair + 1, :, 0:RANK]], axis=1
            )
        for copy in zc_copies:
            copy.start()

    def after_z():
        for copy in zd_copies:
            copy.wait_recv()
        total = zd_ref[0]
        for i in range(1, GY_Z):
            total = total + zd_ref[i]
        g_ref[0] = total
        for copy in g_copies:
            copy.start()

    squares(0, 0, sq_a)

    def body(it, carry):
        position = it * 2

        def at(when, what):
            pl.when(it == when)(what)

        at(X_STEP, after_x)
        at(Z_STEP, after_z)
        at(10, take_meta)
        for m, when in enumerate((11, 14, 17, 19, 20, 21)):
            at(when, functools.partial(take_values, m))
        for m, when in enumerate((15, 17, 19, 21, 22, 22)):
            at(when, ret_copies[m].start)

        a0, b0, self0 = pair_of(position - 1)
        a1, b1, self1 = pair_of(position)
        a2, b2, _ = pair_of(position + 1)
        a3, b3, _ = pair_of(position + 2)
        squares(a2, b2, sq_b)
        tile(sq_a, hi_a, lo_a)
        uses(a0, b0, self0, hi_b, lo_b)
        squares(a3, b3, sq_a)
        tile(sq_b, hi_b, lo_b)
        uses(a1, b1, self1, hi_a, lo_a)
        return carry

    lax.fori_loop(0, TILES // 2, body, 0)
    a0, b0, self0 = pair_of(jnp.int32(TILES - 1))
    uses(a0, b0, self0, hi_b, lo_b)

    for copy in zc_copies:
        copy.wait_recv()
    coupled = jnp.zeros((RHS, RANK), F32)
    for k in range(4):
        partner = clist_ref[0, k]
        used = jnp.where(partner >= 0, 1.0, 0.0)
        place = jnp.maximum(partner, 0)
        slot_z = lax.rem(z_pos + GY_Z - lax.div(place, GX_X), GY_Z)
        slot_x = lax.rem(x_pos + GX_X - lax.rem(place, GX_X), GX_X)
        row = zc_ref[slot_z, lax.div(slot_x, 2)]
        odd = lax.rem(slot_x, 2).astype(F32)
        chosen = row[:, 0:RANK] * ((1.0 - odd) * used) + row[:, RANK : 2 * RANK] * (odd * used)
        coupled = coupled + product(halves(chosen), halves(coup_ref[0, k]), mm)

    for copy in g_copies:
        copy.wait_recv()
    field = jnp.zeros((RHS, RANK), F32)
    for h in range(GX):
        slot = lax.rem(gx + GX - h, GX)
        gap = lax.max(gx - h, h - gx)
        far = jnp.where(gap >= 2, 1.0, 0.0)
        field = field + product(halves(g_ref[slot] * far), halves(top_ref[0, h]), mm)
    cluster = coupled + product(halves(field), halves(ct_ref[0]), mt)
    cluster = halves(cluster)
    for t in range(OWN):
        cols = slice(t * LEAF, (t + 1) * LEAF)
        leaf_field = product(cluster, halves(lt_ref[t]), mt)
        far_values = product(halves(leaf_field), (base_hi[:, cols], base_lo[:, cols]), mm)
        near_sums = acc_ref[t]
        if t < REACH:
            ret_copies[t].wait_recv()
            near_sums = near_sums + ret_ref[t]
        out_ref[:, cols] = near_sums * OUT_SCALE + far_values

    for copy in [pts_copy, list_copy] + halo_copies + ret_copies + x_copies + zd_copies + zc_copies + g_copies:
        copy.wait_send()


def per_device(*arrays):
    rhs_values = arrays[0]
    vmem = pl.BlockSpec(memory_space=pltpu.VMEM)
    smem = pl.BlockSpec(memory_space=pltpu.SMEM)
    dma = pltpu.SemaphoreType.DMA
    return pl.pallas_call(
        kernel,
        out_shape=jax.ShapeDtypeStruct(rhs_values.shape, F32),
        in_specs=[vmem] * 6 + [smem] + [vmem] * 2,
        out_specs=vmem,
        scratch_shapes=[
            pltpu.VMEM((TABLE, 8, LEAF), F32),
            pltpu.VMEM((OWN, 8, LEAF), F32),
            pltpu.VMEM((OWN, LEAF, 128), BF16),
            pltpu.VMEM((TABLE, 2 * RHS, LEAF), BF16),
            pltpu.VMEM((TABLE, RHS, LEAF), F32),
            pltpu.VMEM((2 * REACH + 2, 2 * OWN, LEAF), F32),
            pltpu.VMEM((RANK, OWN * LEAF), BF16),
            pltpu.VMEM((RANK, OWN * LEAF), BF16),
            pltpu.VMEM((LEAF, LEAF), F32),
            pltpu.VMEM((LEAF, LEAF), F32),
            pltpu.VMEM((LEAF, LEAF), BF16),
            pltpu.VMEM((LEAF, LEAF), BF16),
            pltpu.VMEM((LEAF, LEAF), BF16),
            pltpu.VMEM((LEAF, LEAF), BF16),
            pltpu.VMEM((REACH, RHS, LEAF), F32),
            pltpu.VMEM((3, REACH * LEAF), F32),
            pltpu.VMEM((OWN, NEAR), jnp.int32),
            pltpu.VMEM((REACH, RHS, LEAF), F32),
            pltpu.VMEM((GX_X, RHS, 2 * RANK), F32),
            pltpu.VMEM((GY_Z, RHS, RANK), F32),
            pltpu.VMEM((GY_Z, 2, RHS, 2 * RANK), F32),
            pltpu.VMEM((GX, RHS, RANK), F32),
            dma((REACH,)),
            dma((REACH,)),
            dma((2,)),
            dma((2,)),
            dma((REACH,)),
            dma((REACH,)),
            dma((GX_X - 1,)),
            dma((GX_X - 1,)),
            dma((GY_Z - 1,)),
            dma((GY_Z - 1,)),
            dma((GY_Z - 1,)),
            dma((GY_Z - 1,)),
            dma((GX - 1,)),
            dma((GX - 1,)),
        ],
        compiler_params=pltpu.CompilerParams(collective_id=0, has_side_effects=True),
        name="h2_product",
    )(*arrays)


def solution(mesh):
    return jax.shard_map(
        per_device,
        mesh=mesh,
        in_specs=(
            P(None, ("gx", "gy")),
            P(None, ("gx", "gy")),
            P(None, ("gx", "gy")),
            P(("gx", "gy"), None, None),
            P(("gx", "gy"), None, None),
            P(("gx", "gy"), None),
            P(("gx", "gy"), None),
            P(("gx", "gy"), None, None, None),
            P("gx", None, None, None),
        ),
        out_specs=P(None, ("gx", "gy")),
        check_vma=False,
    )
```

time: 210 us -> 38.2 us (0.18)
  matrix products: 137 us -> 0 us
  Pallas kernels: 0 us -> 36.4 us
  starting transfers between devices: 30.9 us -> 0 us
  local copies, waits for them, and re-layouts: 21.1 us -> 1.67 us
  waiting for transfers between devices: 14 us -> 0 us
  other arithmetic: 4.69 us -> 0 us
    dot_general x21 -> x0, matrix products: 137 us -> none  [the longest x12 134 us: add_slot(): jnp.einsum('rlj,lji->rli', source_vals, tile, precision=precise)]
    pallas_call x0 -> x1, Pallas kernels: none -> 36.4 us  [per_device(): pl.pallas_call(kernel, out_shape=jax.ShapeDtypeStruct(rhs_values.shape, F...]
    all_to_all x3 -> x0, starting transfers between devices: 17.9 us -> none  [from_everyone(): lax.all_to_all(jnp.broadcast_to(array[None], (devices, *array.shape)), ax...]
    gather x24 -> x0, local copies, waits for them, and re-layouts: 13.7 us -> none  [the longest x12 6.92 us: add_slot(): source_pts = jnp.take(source_pts_all, column, axis=1)]
    all_to_all x3 -> x0, waiting for transfers between devices: 13 us -> none  [from_everyone(): lax.all_to_all(jnp.broadcast_to(array[None], (devices, *array.shape)), ax...]
    ppermute x2 -> x0, starting transfers between devices: 13 us -> none  [passed_along(): return lax.ppermute(array, axis, pairs)]
    all_to_all x3 -> x0, other arithmetic: 3.39 us -> none  [from_everyone(): lax.all_to_all(jnp.broadcast_to(array[None], (devices, *array.shape)), ax...]
    unnamed x27 -> x1, local copies, waits for them, and re-layouts: 4.48 us -> 1.67 us
  transfers between devices with their start and end apart: 5 -> 0, of which waited for: 3 -> 0; matrix products, arithmetic and copies ran while one was open for 74% -> 0% of each run, Pallas kernels for 0% -> 0%
where the time goes in v1:
time: 38.2 us; the launch traced here: 38.1 us
  Pallas kernels  36.4 us (95%)
  local copies, waits for them, and re-layouts  1.67 us (4%)
    pallas_call x1, Pallas kernels, per_device(): pl.pallas_call(kernel, out_shape=jax.ShapeDtypeStruct(rhs_values.shape, F...  36.4 us
    unnamed x1, local copies, waits for them, and re-layouts  1.67 us

profile of v1, /device:TPU:1, one launch (start us, length us, event | category | flops | bytes accessed | tf_op | source)
XLA Modules:
  0.0 38.1 jit_solution(11937673988356793432)
XLA Ops:
  0.0 36.4 %h2_product.1 = f32[32,2048]{1,0:T(8,128)} custom-call(f32[32,2048]{1,0:T(8,128)} %rhs_ref.1, f32[3,2048]{1,0:T(4,128)} %pts_ref.1, f32[64,2048]{1,0:T(8,128)} %basis_ref.1, f32[8,64,64]{2,1,0:T(8,128)} %lt_ref.1, f32[1,64,64]{2,1,0:T(8,128)} %ct_ref.1, s32[8,12]{1,0:T(8,128)} %near_ref.1, s32[1,4]{1,0:T(1,128)} %clist_ref.1, f32[1,4,64,64]{3,2,1,0:T(8,128)} %coup_ref.1, ...), custom_call_target="tpu_custom_call" | custom-call | tf_op jit(solution)/shard_map/h2_product/pallas_call | solution.py:414
  36.4 1.7 %copy.11 = f32[32,2048]{1,0:T(8,128)} copy(f32[32,2048]{1,0:T(8,128)} %h2_product.1) | data formatting | bytes 524288

commit v2 on v1

--- a/solution.py
+++ b/solution.py
@@ -34,11 +34,13 @@
 OUT_SCALE = COS_SCALE * TURNS * 0.03 * (NEAR * LEAF) ** (-0.5)
 TINY = 1e-30
 
-FIRST = 22
 CROSS = 21
 TILES = 56
-X_STEP = 7
-Z_STEP = 19
+CROSS_STEP = 12
+CROSS_STEP_LATE = 16
+X_STEP = 4
+Z_STEP = 20
+Z_GAP = 4
 
 
 def halves(value):
@@ -73,38 +75,53 @@
     return lax.div(position - threshold + 64, 64)
 
 
-def pair_of(position):
+def pair_of(position, first):
     position = jnp.minimum(jnp.maximum(position, 0), TILES - 1)
     past_self = step_at(position, OWN)
-    past_first = step_at(position, FIRST)
-    past_cross = step_at(position, FIRST + CROSS)
+    past_first = step_at(position, first)
+    past_cross = step_at(position, first + CROSS)
     crossing = past_first - past_cross
     other = past_self - crossing
     queue = lax.max(position - OWN - CROSS * past_cross + 4, 0)
     lag = 4 - lax.div(queue, 8)
     own_a = lax.rem(queue, 8)
     own_b = lax.rem(own_a + lag, 8)
-    count = position - FIRST
+    count = position - first
     halo = step_at(count, 6) + step_at(count, 11) + step_at(count, 15) + step_at(count, 18) + step_at(count, 20)
-    cross_a = count - lax.div(13 * halo - halo * halo, 2) + halo + 2
+    cross_a = count - lax.div(13 * halo - halo * halo, 2)
     cross_b = OWN + halo
     at_self = 1 - past_self
     a = at_self * position + other * own_a + crossing * cross_a
     b = at_self * position + other * own_b + crossing * cross_b
-    return a, b, at_self
+    return a, b, at_self, crossing
 
 
 def kernel(
+    rhs_hbm,
+    pts_hbm,
+    basis_hbm,
+    lt_hbm,
+    ct_hbm,
+    near_hbm,
+    clist_ref,
+    coup_hbm,
+    top_hbm,
+    out_ref,
     rhs_ref,
     pts_ref,
     basis_ref,
     lt_ref,
     ct_ref,
     near_ref,
-    clist_ref,
     coup_ref,
     top_ref,
-    out_ref,
+    lt_hi,
+    lt_lo,
+    top_hi,
+    top_lo,
+    coup_hi,
+    coup_lo,
+    load_sem,
     xy_ref,
     centre_ref,
     left_ref,
@@ -142,6 +159,16 @@
     g_send,
     g_recv,
 ):
+    loads = [
+        pltpu.make_async_copy(src, dst, load_sem.at[i])
+        for i, (src, dst) in enumerate(
+            [(rhs_hbm, rhs_ref), (basis_hbm, basis_ref), (lt_hbm, lt_ref), (ct_hbm, ct_ref), (pts_hbm, pts_ref),
+             (near_hbm, near_ref), (coup_hbm, coup_ref), (top_hbm, top_ref)]
+        )
+    ]
+    for load in loads:
+        load.start()
+
     gx = lax.axis_index("gx")
     gy = lax.axis_index("gy")
     x_pos = lax.rem(gy, GX_X)
@@ -160,22 +187,31 @@
         )
 
     barrier = pltpu.get_barrier_semaphore()
-    greeted = [following, previous] + x_peers + z_peers + g_peers
+    greeted = [previous] + x_peers + g_peers
     for device in greeted:
         pl.semaphore_signal(barrier, inc=1, device_id=device, device_id_type=MESH)
+    for i in range(1, GY_Z):
+
+        @pl.when(z_pos + i < GY_Z)
+        def _(i=i):
+            pl.semaphore_signal(barrier, inc=1, device_id=z_peers[i - 1], device_id_type=MESH)
 
     pts_copy = remote(
-        pts_ref.at[:, pl.ds(0, REACH * LEAF)], halo_pts, meta_send.at[0], meta_recv.at[0], previous
+        pts_ref.at[:, pl.ds(2 * LEAF, REACH * LEAF)], halo_pts, meta_send.at[0], meta_recv.at[0], following
     )
-    list_copy = remote(near_ref, halo_list, meta_send.at[1], meta_recv.at[1], previous)
+    list_copy = remote(near_ref, halo_list, meta_send.at[1], meta_recv.at[1], following)
     halo_copies = [
         remote(
-            rhs_ref.at[:, pl.ds(m * LEAF, LEAF)], halo_vals.at[m], halo_send.at[m], halo_recv.at[m], previous
+            rhs_ref.at[:, pl.ds((OWN - 1 - m) * LEAF, LEAF)],
+            halo_vals.at[m],
+            halo_send.at[m],
+            halo_recv.at[m],
+            following,
         )
         for m in range(REACH)
     ]
     ret_copies = [
-        remote(acc_ref.at[OWN + m], ret_ref.at[m], ret_send.at[m], ret_recv.at[m], following)
+        remote(acc_ref.at[OWN + m], ret_ref.at[m], ret_send.at[m], ret_recv.at[m], previous)
         for m in range(REACH)
     ]
     x_copies = [
@@ -211,27 +247,35 @@
         vals_ref[slot, 0:RHS, :] = high
         vals_ref[slot, RHS : 2 * RHS, :] = low
 
-    pl.semaphore_wait(barrier, len(greeted))
-    pts_copy.start()
-    list_copy.start()
-    for copy in halo_copies:
-        copy.start()
-
+    loads[0].wait()
     for t in range(OWN):
         store_values(t, rhs_ref[:, t * LEAF : (t + 1) * LEAF])
+    loads[1].wait()
     high, low = halves(basis_ref[...])
     base_hi[...] = high
     base_lo[...] = low
+    loads[2].wait()
+    high, low = halves(lt_ref[...])
+    lt_hi[...] = high
+    lt_lo[...] = low
     own_coeffs = jnp.zeros((RHS, RANK), F32)
     for t in range(OWN):
         cols = slice(t * LEAF, (t + 1) * LEAF)
         both = mt(vals_ref[t], base_hi[:, cols])
         leaf_coeffs = both[0:RHS] + both[RHS:] + mt(vals_ref[t, 0:RHS, :], base_lo[:, cols])
-        own_coeffs = own_coeffs + product(halves(leaf_coeffs), halves(lt_ref[t]), mm)
+        own_coeffs = own_coeffs + product(halves(leaf_coeffs), (lt_hi[t], lt_lo[t]), mm)
+    loads[3].wait()
     own_terms = product(halves(own_coeffs), halves(ct_ref[0]), mm)
     x_ref[0, :, 0:RANK] = own_coeffs
     x_ref[0, :, RANK : 2 * RANK] = own_terms
+    loads[4].wait()
+    loads[5].wait()
+    pl.semaphore_wait(barrier, len(greeted) + z_pos)
     for copy in x_copies:
+        copy.start()
+    pts_copy.start()
+    list_copy.start()
+    for copy in halo_copies:
         copy.start()
 
     xy_ref[...] = jnp.zeros_like(xy_ref)
@@ -286,10 +330,12 @@
             into_hi[rows, :] = high
             into_lo[rows, :] = (value - high.astype(F32)).astype(BF16)
 
-    def uses(a, b, at_self, from_hi, from_lo):
+    def uses(pair, from_hi, from_lo):
+        a, b, at_self, crossing = pair
         high, low = from_hi[...], from_lo[...]
-        offset = b - a
-        mask_b = mask_ref[REACH - offset + (REACH + 1 + offset) * at_self, pl.ds(b, 1), :]
+        offset = (1 - crossing) * (b - a) + crossing * (OWN - 1 - b - a)
+        row = (1 - crossing) * b + crossing * (3 * OWN - 1 - b)
+        mask_b = mask_ref[REACH - offset + (REACH + 1 + offset) * at_self, pl.ds(row, 1), :]
         mask_a = mask_ref[REACH + offset, pl.ds(a, 1), :]
         vals_a = vals_ref[a]
         vals_b = vals_ref[b]
@@ -304,8 +350,9 @@
         pts_copy.wait_recv()
         list_copy.wait_recv()
         for m in range(REACH):
-            xy_ref[OWN + m, 0:3, :] = halo_pts[:, m * LEAF : (m + 1) * LEAF]
-        for index, found in enumerate(masks_from(halo_list[...], first_leaf + OWN)):
+            cols = slice((REACH - 1 - m) * LEAF, (REACH - m) * LEAF)
+            xy_ref[OWN + m, 0:3, :] = halo_pts[:, cols]
+        for index, found in enumerate(masks_from(halo_list[...], first_leaf - OWN)):
             mask_ref[index, OWN : 2 * OWN, :] = found
 
     def take_values(m):
@@ -317,18 +364,24 @@
             copy.wait_recv()
         terms = (x_ref[0] + x_ref[1]) + (x_ref[2] + x_ref[3])
         zd_ref[0] = terms[:, RANK : 2 * RANK]
-        for copy in zd_copies:
-            copy.start()
         for pair in range(2):
             zc_ref[0, pair] = jnp.concatenate(
                 [x_ref[2 * pair, :, 0:RANK], x_ref[2 * pair + 1, :, 0:RANK]], axis=1
             )
-        for copy in zc_copies:
-            copy.start()
-
-    def after_z():
-        for copy in zd_copies:
-            copy.wait_recv()
+        for copies in (zd_copies, zc_copies):
+            for i in range(1, GY_Z):
+                pl.when(z_pos + i >= GY_Z)(copies[i - 1].start)
+
+    def after_high():
+        for i in range(1, GY_Z):
+            pl.when(i > z_pos)(zd_copies[i - 1].wait_recv)
+        for copies in (zd_copies, zc_copies):
+            for i in range(1, GY_Z):
+                pl.when(z_pos + i < GY_Z)(copies[i - 1].start)
+
+    def after_low():
+        for i in range(1, GY_Z):
+            pl.when(i <= z_pos)(zd_copies[i - 1].wait_recv)
         total = zd_ref[0]
         for i in range(1, GY_Z):
             total = total + zd_ref[i]
@@ -336,6 +389,12 @@
         for copy in g_copies:
             copy.start()
 
+    late = lax.div(GY - gy, GY)
+    cross_step = CROSS_STEP + (CROSS_STEP_LATE - CROSS_STEP) * late
+    first = 2 * cross_step
+    high_step = Z_STEP - lax.div(7 * z_pos, 4)
+    low_step = high_step + Z_GAP
+
     squares(0, 0, sq_a)
 
     def body(it, carry):
@@ -345,29 +404,32 @@
             pl.when(it == when)(what)
 
         at(X_STEP, after_x)
-        at(Z_STEP, after_z)
-        at(10, take_meta)
-        for m, when in enumerate((11, 14, 17, 19, 20, 21)):
-            at(when, functools.partial(take_values, m))
-        for m, when in enumerate((15, 17, 19, 21, 22, 22)):
-            at(when, ret_copies[m].start)
-
-        a0, b0, self0 = pair_of(position - 1)
-        a1, b1, self1 = pair_of(position)
-        a2, b2, _ = pair_of(position + 1)
-        a3, b3, _ = pair_of(position + 2)
-        squares(a2, b2, sq_b)
+        at(high_step, after_high)
+        at(low_step, after_low)
+        at(cross_step - 1, take_meta)
+        for m, after in enumerate((0, 3, 6, 8, 9, 10)):
+            at(cross_step + after, functools.partial(take_values, m))
+        for m, after in enumerate((4, 6, 8, 10, 11, 11)):
+            at(cross_step + after, ret_copies[m].start)
+
+        before, this = pair_of(position - 1, first), pair_of(position, first)
+        second, third = pair_of(position + 1, first), pair_of(position + 2, first)
+        squares(second[0], second[1], sq_b)
         tile(sq_a, hi_a, lo_a)
-        uses(a0, b0, self0, hi_b, lo_b)
-        squares(a3, b3, sq_a)
+        uses(before, hi_b, lo_b)
+        squares(third[0], third[1], sq_a)
         tile(sq_b, hi_b, lo_b)
-        uses(a1, b1, self1, hi_a, lo_a)
+        uses(this, hi_a, lo_a)
         return carry
 
     lax.fori_loop(0, TILES // 2, body, 0)
-    a0, b0, self0 = pair_of(jnp.int32(TILES - 1))
-    uses(a0, b0, self0, hi_b, lo_b)
-
+    uses(pair_of(jnp.int32(TILES - 1), first), hi_b, lo_b)
+
+    loads[6].wait()
+    loads[7].wait()
+    top_hi[...], top_lo[...] = halves(top_ref[0])
+    coup_hi[...], coup_lo[...] = halves(coup_ref[0])
+    ct_halves = halves(ct_ref[0])
     for copy in zc_copies:
         copy.wait_recv()
     coupled = jnp.zeros((RHS, RANK), F32)
@@ -380,7 +442,7 @@
         row = zc_ref[slot_z, lax.div(slot_x, 2)]
         odd = lax.rem(slot_x, 2).astype(F32)
         chosen = row[:, 0:RANK] * ((1.0 - odd) * used) + row[:, RANK : 2 * RANK] * (odd * used)
-        coupled = coupled + product(halves(chosen), halves(coup_ref[0, k]), mm)
+        coupled = coupled + product(halves(chosen), (coup_hi[k], coup_lo[k]), mm)
 
     for copy in g_copies:
         copy.wait_recv()
@@ -389,17 +451,17 @@
         slot = lax.rem(gx + GX - h, GX)
         gap = lax.max(gx - h, h - gx)
         far = jnp.where(gap >= 2, 1.0, 0.0)
-        field = field + product(halves(g_ref[slot] * far), halves(top_ref[0, h]), mm)
-    cluster = coupled + product(halves(field), halves(ct_ref[0]), mt)
+        field = field + product(halves(g_ref[slot] * far), (top_hi[h], top_lo[h]), mm)
+    cluster = coupled + product(halves(field), ct_halves, mt)
     cluster = halves(cluster)
     for t in range(OWN):
         cols = slice(t * LEAF, (t + 1) * LEAF)
-        leaf_field = product(cluster, halves(lt_ref[t]), mt)
+        leaf_field = product(cluster, (lt_hi[t], lt_lo[t]), mt)
         far_values = product(halves(leaf_field), (base_hi[:, cols], base_lo[:, cols]), mm)
         near_sums = acc_ref[t]
-        if t < REACH:
-            ret_copies[t].wait_recv()
-            near_sums = near_sums + ret_ref[t]
+        if t >= OWN - REACH:
+            ret_copies[OWN - 1 - t].wait_recv()
+            near_sums = near_sums + ret_ref[OWN - 1 - t]
         out_ref[:, cols] = near_sums * OUT_SCALE + far_values
 
     for copy in [pts_copy, list_copy] + halo_copies + ret_copies + x_copies + zd_copies + zc_copies + g_copies:
@@ -409,14 +471,30 @@
 def per_device(*arrays):
     rhs_values = arrays[0]
     vmem = pl.BlockSpec(memory_space=pltpu.VMEM)
+    anywhere = pl.BlockSpec(memory_space=pl.ANY)
     smem = pl.BlockSpec(memory_space=pltpu.SMEM)
     dma = pltpu.SemaphoreType.DMA
     return pl.pallas_call(
         kernel,
         out_shape=jax.ShapeDtypeStruct(rhs_values.shape, F32),
-        in_specs=[vmem] * 6 + [smem] + [vmem] * 2,
+        in_specs=[anywhere] * 6 + [smem] + [anywhere] * 2,
         out_specs=vmem,
         scratch_shapes=[
+            pltpu.VMEM((RHS, OWN * LEAF), F32),
+            pltpu.VMEM((3, OWN * LEAF), F32),
+            pltpu.VMEM((RANK, OWN * LEAF), F32),
+            pltpu.VMEM((OWN, RANK, RANK), F32),
+            pltpu.VMEM((1, RANK, RANK), F32),
+            pltpu.VMEM((OWN, NEAR), jnp.int32),
+            pltpu.VMEM((1, 4, RANK, RANK), F32),
+            pltpu.VMEM((1, GX, RANK, RANK), F32),
+            pltpu.VMEM((OWN, RANK, RANK), BF16),
+            pltpu.VMEM((OWN, RANK, RANK), BF16),
+            pltpu.VMEM((GX, RANK, RANK), BF16),
+            pltpu.VMEM((GX, RANK, RANK), BF16),
+            pltpu.VMEM((4, RANK, RANK), BF16),
+            pltpu.VMEM((4, RANK, RANK), BF16),
+            dma((8,)),
             pltpu.VMEM((TABLE, 8, LEAF), F32),
             pltpu.VMEM((OWN, 8, LEAF), F32),
             pltpu.VMEM((OWN, LEAF, 128), BF16),

time: 38.2 us -> 45 us (1.18)
  the two profiles are of different devices: /device:TPU:1 before, /device:TPU:192 now
where the time goes in v2:
time: 45 us; the launch traced here: 44.8 us
  Pallas kernels  43.1 us (96%)
  local copies, waits for them, and re-layouts  1.67 us (4%)
    pallas_call x1, Pallas kernels, per_device(): pl.pallas_call(kernel, out_shape=jax.ShapeDtypeStruct(rhs_values.shape, F...  43.1 us
    unnamed x1, local copies, waits for them, and re-layouts  1.67 us

profile of v2, /device:TPU:192, one launch (start us, length us, event | category | flops | bytes accessed | tf_op | source)
XLA Modules:
  0.0 44.8 jit_solution(5698337852615510757)
XLA Ops:
  0.0 43.1 %h2_product.1 = f32[32,2048]{1,0:T(8,128)} custom-call(f32[32,2048]{1,0:T(8,128)} %rhs_hbm.1, f32[3,2048]{1,0:T(4,128)} %pts_hbm.1, f32[64,2048]{1,0:T(8,128)} %basis_hbm.1, f32[8,64,64]{2,1,0:T(8,128)} %lt_hbm.1, f32[1,64,64]{2,1,0:T(8,128)} %ct_hbm.1, s32[8,12]{1,0:T(8,128)} %near_hbm.1, s32[1,4]{1,0:T(1,128)} %clist_ref.1, f32[1,4,64,64]{3,2,1,0:T(8,128)} %coup_hbm.1, ...), custom_call_target="tpu_custom_call" | custom-call | tf_op jit(solution)/shard_map/h2_product/pallas_call | solution.py:477
  43.2 1.7 %copy.11 = f32[32,2048]{1,0:T(8,128)} copy(f32[32,2048]{1,0:T(8,128)} %h2_product.1) | data formatting | bytes 524288

commit v3 on v2

--- a/solution.py
+++ b/solution.py
@@ -36,11 +36,11 @@
 
 CROSS = 21
 TILES = 56
-CROSS_STEP = 12
+CROSS_STEP = 11
 CROSS_STEP_LATE = 16
-X_STEP = 4
-Z_STEP = 20
-Z_GAP = 4
+HIGH_STEP = 14
+LOW_STEP = 16
+X_STEP = 22
 
 
 def halves(value):
@@ -140,9 +140,9 @@
     halo_pts,
     halo_list,
     ret_ref,
-    x_ref,
-    zd_ref,
-    zc_ref,
+    z_ref,
+    xd_ref,
+    xc_ref,
     g_ref,
     halo_send,
     halo_recv,
@@ -150,12 +150,12 @@
     meta_recv,
     ret_send,
     ret_recv,
-    x_send,
-    x_recv,
-    zd_send,
-    zd_recv,
-    zc_send,
-    zc_recv,
+    z_send,
+    z_recv,
+    xd_send,
+    xd_recv,
+    xc_send,
+    xc_recv,
     g_send,
     g_recv,
 ):
@@ -214,17 +214,17 @@
         remote(acc_ref.at[OWN + m], ret_ref.at[m], ret_send.at[m], ret_recv.at[m], previous)
         for m in range(REACH)
     ]
-    x_copies = [
-        remote(x_ref.at[0], x_ref.at[i], x_send.at[i - 1], x_recv.at[i - 1], x_peers[i - 1])
+    z_copies = [
+        remote(z_ref.at[0], z_ref.at[i], z_send.at[i - 1], z_recv.at[i - 1], z_peers[i - 1])
+        for i in range(1, GY_Z)
+    ]
+    xd_copies = [
+        remote(xd_ref.at[0], xd_ref.at[i], xd_send.at[i - 1], xd_recv.at[i - 1], x_peers[i - 1])
         for i in range(1, GX_X)
     ]
-    zd_copies = [
-        remote(zd_ref.at[0], zd_ref.at[i], zd_send.at[i - 1], zd_recv.at[i - 1], z_peers[i - 1])
-        for i in range(1, GY_Z)
-    ]
-    zc_copies = [
-        remote(zc_ref.at[0], zc_ref.at[i], zc_send.at[i - 1], zc_recv.at[i - 1], z_peers[i - 1])
-        for i in range(1, GY_Z)
+    xc_copies = [
+        remote(xc_ref.at[0], xc_ref.at[i], xc_send.at[i - 1], xc_recv.at[i - 1], x_peers[i - 1])
+        for i in range(1, GX_X)
     ]
     g_copies = [
         remote(g_ref.at[0], g_ref.at[i], g_send.at[i - 1], g_recv.at[i - 1], g_peers[i - 1])
@@ -266,17 +266,19 @@
         own_coeffs = own_coeffs + product(halves(leaf_coeffs), (lt_hi[t], lt_lo[t]), mm)
     loads[3].wait()
     own_terms = product(halves(own_coeffs), halves(ct_ref[0]), mm)
-    x_ref[0, :, 0:RANK] = own_coeffs
-    x_ref[0, :, RANK : 2 * RANK] = own_terms
+    z_ref[0, :, 0:RANK] = own_coeffs
+    z_ref[0, :, RANK : 2 * RANK] = own_terms
     loads[4].wait()
     loads[5].wait()
-    pl.semaphore_wait(barrier, len(greeted) + z_pos)
-    for copy in x_copies:
-        copy.start()
-    pts_copy.start()
-    list_copy.start()
-    for copy in halo_copies:
-        copy.start()
+
+    def begin():
+        pl.semaphore_wait(barrier, len(greeted) + z_pos)
+        for i in range(1, GY_Z):
+            pl.when(z_pos + i >= GY_Z)(z_copies[i - 1].start)
+        pts_copy.start()
+        list_copy.start()
+        for copy in halo_copies:
+            copy.start()
 
     xy_ref[...] = jnp.zeros_like(xy_ref)
     for t in range(OWN):
@@ -359,78 +361,94 @@
         halo_copies[m].wait_recv()
         store_values(OWN + m, halo_vals[m])
 
-    def after_x():
-        for copy in x_copies:
-            copy.wait_recv()
-        terms = (x_ref[0] + x_ref[1]) + (x_ref[2] + x_ref[3])
-        zd_ref[0] = terms[:, RANK : 2 * RANK]
-        for pair in range(2):
-            zc_ref[0, pair] = jnp.concatenate(
-                [x_ref[2 * pair, :, 0:RANK], x_ref[2 * pair + 1, :, 0:RANK]], axis=1
-            )
-        for copies in (zd_copies, zc_copies):
-            for i in range(1, GY_Z):
-                pl.when(z_pos + i >= GY_Z)(copies[i - 1].start)
-
     def after_high():
         for i in range(1, GY_Z):
-            pl.when(i > z_pos)(zd_copies[i - 1].wait_recv)
-        for copies in (zd_copies, zc_copies):
-            for i in range(1, GY_Z):
-                pl.when(z_pos + i < GY_Z)(copies[i - 1].start)
+            pl.when(i > z_pos)(z_copies[i - 1].wait_recv)
+        for i in range(1, GY_Z):
+            pl.when(z_pos + i < GY_Z)(z_copies[i - 1].start)
 
     def after_low():
         for i in range(1, GY_Z):
-            pl.when(i <= z_pos)(zd_copies[i - 1].wait_recv)
-        total = zd_ref[0]
+            pl.when(i <= z_pos)(z_copies[i - 1].wait_recv)
+        terms = z_ref[0, :, RANK : 2 * RANK]
         for i in range(1, GY_Z):
-            total = total + zd_ref[i]
-        g_ref[0] = total
+            terms = terms + z_ref[i, :, RANK : 2 * RANK]
+        half = RHS // 2
+        xd_ref[0] = jnp.concatenate([terms[0:half], terms[half:]], axis=1)
+        for copy in xd_copies:
+            copy.start()
+        for pair in range(GY_Z // 2):
+            xc_ref[0, pair] = jnp.concatenate(
+                [z_ref[2 * pair, :, 0:RANK], z_ref[2 * pair + 1, :, 0:RANK]], axis=1
+            )
+        for copy in xc_copies:
+            copy.start()
+
+    def after_x():
+        for copy in xd_copies:
+            copy.wait_recv()
+        g_ref[0] = (xd_ref[0] + xd_ref[1]) + (xd_ref[2] + xd_ref[3])
         for copy in g_copies:
             copy.start()
 
     late = lax.div(GY - gy, GY)
     cross_step = CROSS_STEP + (CROSS_STEP_LATE - CROSS_STEP) * late
     first = 2 * cross_step
-    high_step = Z_STEP - lax.div(7 * z_pos, 4)
-    low_step = high_step + Z_GAP
+    high_step = HIGH_STEP - 2 * jnp.minimum(z_pos, 4)
 
     squares(0, 0, sq_a)
 
+    def events(it):
+        def at(when, *what):
+            @pl.when(it == when)
+            def _():
+                for each in what:
+                    each()
+
+        def take(m):
+            return functools.partial(take_values, m)
+
+        at(1, begin)
+        at(high_step, after_high)
+
+        at(LOW_STEP, after_low)
+        at(X_STEP, after_x)
+
+        @pl.when((it >= cross_step - 1) & (it <= cross_step + 11))
+        def _():
+            at(cross_step - 1, take_meta)
+            at(cross_step, take(0))
+            at(cross_step + 3, take(1))
+            at(cross_step + 4, ret_copies[0].start)
+            at(cross_step + 6, take(2), ret_copies[1].start)
+            at(cross_step + 8, take(3), ret_copies[2].start)
+            at(cross_step + 9, take(4))
+            at(cross_step + 10, take(5), ret_copies[3].start)
+            at(cross_step + 11, ret_copies[4].start, ret_copies[5].start)
+
     def body(it, carry):
-        position = it * 2
-
-        def at(when, what):
-            pl.when(it == when)(what)
-
-        at(X_STEP, after_x)
-        at(high_step, after_high)
-        at(low_step, after_low)
-        at(cross_step - 1, take_meta)
-        for m, after in enumerate((0, 3, 6, 8, 9, 10)):
-            at(cross_step + after, functools.partial(take_values, m))
-        for m, after in enumerate((4, 6, 8, 10, 11, 11)):
-            at(cross_step + after, ret_copies[m].start)
-
-        before, this = pair_of(position - 1, first), pair_of(position, first)
-        second, third = pair_of(position + 1, first), pair_of(position + 2, first)
+        events(it)
+        before, this, second, third = carry
+        position = it * 2 + 2
+        coming = (second, third, pair_of(position + 1, first), pair_of(position + 2, first))
         squares(second[0], second[1], sq_b)
         tile(sq_a, hi_a, lo_a)
         uses(before, hi_b, lo_b)
         squares(third[0], third[1], sq_a)
         tile(sq_b, hi_b, lo_b)
         uses(this, hi_a, lo_a)
-        return carry
-
-    lax.fori_loop(0, TILES // 2, body, 0)
-    uses(pair_of(jnp.int32(TILES - 1), first), hi_b, lo_b)
+        return coming
+
+    start = tuple(pair_of(jnp.int32(position), first) for position in (-1, 0, 1, 2))
+    before, *_ = lax.fori_loop(0, TILES // 2, body, start)
+    uses(before, hi_b, lo_b)
 
     loads[6].wait()
     loads[7].wait()
     top_hi[...], top_lo[...] = halves(top_ref[0])
     coup_hi[...], coup_lo[...] = halves(coup_ref[0])
     ct_halves = halves(ct_ref[0])
-    for copy in zc_copies:
+    for copy in xc_copies:
         copy.wait_recv()
     coupled = jnp.zeros((RHS, RANK), F32)
     for k in range(4):
@@ -439,8 +457,8 @@
         place = jnp.maximum(partner, 0)
         slot_z = lax.rem(z_pos + GY_Z - lax.div(place, GX_X), GY_Z)
         slot_x = lax.rem(x_pos + GX_X - lax.rem(place, GX_X), GX_X)
-        row = zc_ref[slot_z, lax.div(slot_x, 2)]
-        odd = lax.rem(slot_x, 2).astype(F32)
+        row = xc_ref[slot_x, lax.div(slot_z, 2)]
+        odd = lax.rem(slot_z, 2).astype(F32)
         chosen = row[:, 0:RANK] * ((1.0 - odd) * used) + row[:, RANK : 2 * RANK] * (odd * used)
         coupled = coupled + product(halves(chosen), (coup_hi[k], coup_lo[k]), mm)
 
@@ -451,7 +469,7 @@
         slot = lax.rem(gx + GX - h, GX)
         gap = lax.max(gx - h, h - gx)
         far = jnp.where(gap >= 2, 1.0, 0.0)
-        field = field + product(halves(g_ref[slot] * far), (top_hi[h], top_lo[h]), mm)
+        field = field + product(halves(jnp.concatenate([g_ref[slot, :, 0:RANK], g_ref[slot, :, RANK:]], axis=0) * far), (top_hi[h], top_lo[h]), mm)
     cluster = coupled + product(halves(field), ct_halves, mt)
     cluster = halves(cluster)
     for t in range(OWN):
@@ -464,7 +482,7 @@
             near_sums = near_sums + ret_ref[OWN - 1 - t]
         out_ref[:, cols] = near_sums * OUT_SCALE + far_values
 
-    for copy in [pts_copy, list_copy] + halo_copies + ret_copies + x_copies + zd_copies + zc_copies + g_copies:
+    for copy in [pts_copy, list_copy] + halo_copies + ret_copies + z_copies + xd_copies + xc_copies + g_copies:
         copy.wait_send()
 
 
@@ -513,22 +531,22 @@
             pltpu.VMEM((3, REACH * LEAF), F32),
             pltpu.VMEM((OWN, NEAR), jnp.int32),
             pltpu.VMEM((REACH, RHS, LEAF), F32),
-            pltpu.VMEM((GX_X, RHS, 2 * RANK), F32),
-            pltpu.VMEM((GY_Z, RHS, RANK), F32),
-            pltpu.VMEM((GY_Z, 2, RHS, 2 * RANK), F32),
-            pltpu.VMEM((GX, RHS, RANK), F32),
+            pltpu.VMEM((GY_Z, RHS, 2 * RANK), F32),
+            pltpu.VMEM((GX_X, RHS // 2, 2 * RANK), F32),
+            pltpu.VMEM((GX_X, GY_Z // 2, RHS, 2 * RANK), F32),
+            pltpu.VMEM((GX, RHS // 2, 2 * RANK), F32),
             dma((REACH,)),
             dma((REACH,)),
             dma((2,)),
             dma((2,)),
             dma((REACH,)),
             dma((REACH,)),
+            dma((GY_Z - 1,)),
+            dma((GY_Z - 1,)),
             dma((GX_X - 1,)),
             dma((GX_X - 1,)),
-            dma((GY_Z - 1,)),
-            dma((GY_Z - 1,)),
-            dma((GY_Z - 1,)),
-            dma((GY_Z - 1,)),
+            dma((GX_X - 1,)),
+            dma((GX_X - 1,)),
             dma((GX - 1,)),
             dma((GX - 1,)),
         ],

time: 45 us -> 34 us (0.76)
  the two profiles are of different devices: /device:TPU:192 before, /device:TPU:1 now
where the time goes in v3:
time: 34 us; the launch traced here: 33.8 us
  Pallas kernels  32.2 us (95%)
  local copies, waits for them, and re-layouts  1.67 us (5%)
    pallas_call x1, Pallas kernels, per_device(): pl.pallas_call(kernel, out_shape=jax.ShapeDtypeStruct(rhs_values.shape, F...  32.2 us
    unnamed x1, local copies, waits for them, and re-layouts  1.67 us

profile of v3, /device:TPU:1, one launch (start us, length us, event | category | flops | bytes accessed | tf_op | source)
XLA Modules:
  0.0 33.8 jit_solution(10089033629864137387)
XLA Ops:
  0.0 32.2 %h2_product.1 = f32[32,2048]{1,0:T(8,128)} custom-call(f32[32,2048]{1,0:T(8,128)} %rhs_hbm.1, f32[3,2048]{1,0:T(4,128)} %pts_hbm.1, f32[64,2048]{1,0:T(8,128)} %basis_hbm.1, f32[8,64,64]{2,1,0:T(8,128)} %lt_hbm.1, f32[1,64,64]{2,1,0:T(8,128)} %ct_hbm.1, s32[8,12]{1,0:T(8,128)} %near_hbm.1, s32[1,4]{1,0:T(1,128)} %clist_ref.1, f32[1,4,64,64]{3,2,1,0:T(8,128)} %coup_hbm.1, ...), custom_call_target="tpu_custom_call" | custom-call | tf_op jit(solution)/shard_map/h2_product/pallas_call | solution.py:495
  32.2 1.7 %copy.11 = f32[32,2048]{1,0:T(8,128)} copy(f32[32,2048]{1,0:T(8,128)} %h2_product.1) | data formatting | bytes 524288

commit v4 on v3

--- a/solution.py
+++ b/solution.py
@@ -36,11 +36,11 @@
 
 CROSS = 21
 TILES = 56
-CROSS_STEP = 11
-CROSS_STEP_LATE = 16
-HIGH_STEP = 14
-LOW_STEP = 16
-X_STEP = 22
+CROSS_STEP = 5
+CROSS_STEP_LATE = 7
+HIGH_STEP = 6
+LOW_STEP = 7
+X_STEP = 10
 
 
 def halves(value):
@@ -393,8 +393,8 @@
 
     late = lax.div(GY - gy, GY)
     cross_step = CROSS_STEP + (CROSS_STEP_LATE - CROSS_STEP) * late
-    first = 2 * cross_step
-    high_step = HIGH_STEP - 2 * jnp.minimum(z_pos, 4)
+    first = 4 * cross_step
+    high_step = HIGH_STEP - jnp.minimum(z_pos, 4)
 
     squares(0, 0, sq_a)
 
@@ -408,39 +408,43 @@
         def take(m):
             return functools.partial(take_values, m)
 
-        at(1, begin)
+        at(0, begin)
         at(high_step, after_high)
-
         at(LOW_STEP, after_low)
         at(X_STEP, after_x)
 
-        @pl.when((it >= cross_step - 1) & (it <= cross_step + 11))
+        @pl.when((it >= cross_step - 1) & (it <= cross_step + 6))
         def _():
             at(cross_step - 1, take_meta)
             at(cross_step, take(0))
-            at(cross_step + 3, take(1))
-            at(cross_step + 4, ret_copies[0].start)
-            at(cross_step + 6, take(2), ret_copies[1].start)
-            at(cross_step + 8, take(3), ret_copies[2].start)
-            at(cross_step + 9, take(4))
-            at(cross_step + 10, take(5), ret_copies[3].start)
-            at(cross_step + 11, ret_copies[4].start, ret_copies[5].start)
+            at(cross_step + 1, take(1))
+            at(cross_step + 2, ret_copies[0].start)
+            at(cross_step + 3, take(2), ret_copies[1].start)
+            at(cross_step + 4, take(3), take(4), ret_copies[2].start)
+            at(cross_step + 5, take(5), ret_copies[3].start)
+            at(cross_step + 6, ret_copies[4].start, ret_copies[5].start)
 
     def body(it, carry):
         events(it)
-        before, this, second, third = carry
-        position = it * 2 + 2
-        coming = (second, third, pair_of(position + 1, first), pair_of(position + 2, first))
+        before, this, second, third, fourth, fifth = carry
+        position = it * 4 + 4
+        coming = (fourth, fifth) + tuple(pair_of(position + i, first) for i in range(1, 5))
         squares(second[0], second[1], sq_b)
         tile(sq_a, hi_a, lo_a)
         uses(before, hi_b, lo_b)
         squares(third[0], third[1], sq_a)
         tile(sq_b, hi_b, lo_b)
         uses(this, hi_a, lo_a)
+        squares(fourth[0], fourth[1], sq_b)
+        tile(sq_a, hi_a, lo_a)
+        uses(second, hi_b, lo_b)
+        squares(fifth[0], fifth[1], sq_a)
+        tile(sq_b, hi_b, lo_b)
+        uses(third, hi_a, lo_a)
         return coming
 
-    start = tuple(pair_of(jnp.int32(position), first) for position in (-1, 0, 1, 2))
-    before, *_ = lax.fori_loop(0, TILES // 2, body, start)
+    start = tuple(pair_of(jnp.int32(position), first) for position in range(-1, 5))
+    before, *_ = lax.fori_loop(0, TILES // 4, body, start)
     uses(before, hi_b, lo_b)
 
     loads[6].wait()

time: 34 us -> 33.8 us (level)
  no operation moved by 1% of the time
where the time goes in v4:
time: 33.8 us; the launch traced here: 33.7 us
  Pallas kernels  32 us (95%)
  local copies, waits for them, and re-layouts  1.67 us (5%)
    pallas_call x1, Pallas kernels, per_device(): pl.pallas_call(kernel, out_shape=jax.ShapeDtypeStruct(rhs_values.shape, F...  32 us
    unnamed x1, local copies, waits for them, and re-layouts  1.67 us

profile of v4, /device:TPU:1, one launch (start us, length us, event | category | flops | bytes accessed | tf_op | source)
XLA Modules:
  0.0 33.7 jit_solution(6467249470792466620)
XLA Ops:
  0.0 32.0 %h2_product.1 = f32[32,2048]{1,0:T(8,128)} custom-call(f32[32,2048]{1,0:T(8,128)} %rhs_hbm.1, f32[3,2048]{1,0:T(4,128)} %pts_hbm.1, f32[64,2048]{1,0:T(8,128)} %basis_hbm.1, f32[8,64,64]{2,1,0:T(8,128)} %lt_hbm.1, f32[1,64,64]{2,1,0:T(8,128)} %ct_hbm.1, s32[8,12]{1,0:T(8,128)} %near_hbm.1, s32[1,4]{1,0:T(1,128)} %clist_ref.1, f32[1,4,64,64]{3,2,1,0:T(8,128)} %coup_hbm.1, ...), custom_call_target="tpu_custom_call" | custom-call | tf_op jit(solution)/shard_map/h2_product/pallas_call | solution.py:499
  32.0 1.7 %copy.11 = f32[32,2048]{1,0:T(8,128)} copy(f32[32,2048]{1,0:T(8,128)} %h2_product.1) | data formatting | bytes 524288

commit v5 on v4

--- a/solution.py
+++ b/solution.py
@@ -37,7 +37,7 @@
 CROSS = 21
 TILES = 56
 CROSS_STEP = 5
-CROSS_STEP_LATE = 7
+CROSS_STEP_LATE = 8
 HIGH_STEP = 6
 LOW_STEP = 7
 X_STEP = 10
@@ -394,6 +394,7 @@
     late = lax.div(GY - gy, GY)
     cross_step = CROSS_STEP + (CROSS_STEP_LATE - CROSS_STEP) * late
     first = 4 * cross_step
+    begin_step = 1 - lax.div(jnp.minimum(z_pos, 4), 4)
     high_step = HIGH_STEP - jnp.minimum(z_pos, 4)
 
     squares(0, 0, sq_a)
@@ -408,7 +409,7 @@
         def take(m):
             return functools.partial(take_values, m)
 
-        at(0, begin)
+        at(begin_step, begin)
         at(high_step, after_high)
         at(LOW_STEP, after_low)
         at(X_STEP, after_x)
@@ -446,6 +447,11 @@
     start = tuple(pair_of(jnp.int32(position), first) for position in range(-1, 5))
     before, *_ = lax.fori_loop(0, TILES // 4, body, start)
     uses(before, hi_b, lo_b)
+
+    @pl.when(cross_step + 6 >= TILES // 4)
+    def _():
+        ret_copies[4].start()
+        ret_copies[5].start()
 
     loads[6].wait()
     loads[7].wait()

time: 33.8 us -> 33.4 us (0.988)
  Pallas kernels: 32 us -> 31.6 us
    pallas_call x1, Pallas kernels: 32 us -> 31.6 us  [per_device(): pl.pallas_call(kernel, out_shape=jax.ShapeDtypeStruct(rhs_values.shape, F...]
where the time goes in v5:
time: 33.4 us; the launch traced here: 33.2 us
  Pallas kernels  31.6 us (95%)
  local copies, waits for them, and re-layouts  1.67 us (5%)
    pallas_call x1, Pallas kernels, per_device(): pl.pallas_call(kernel, out_shape=jax.ShapeDtypeStruct(rhs_values.shape, F...  31.6 us
    unnamed x1, local copies, waits for them, and re-layouts  1.67 us

profile of v5, /device:TPU:1, one launch (start us, length us, event | category | flops | bytes accessed | tf_op | source)
XLA Modules:
  0.0 33.2 jit_solution(10483880734748120904)
XLA Ops:
  0.0 31.6 %h2_product.1 = f32[32,2048]{1,0:T(8,128)} custom-call(f32[32,2048]{1,0:T(8,128)} %rhs_hbm.1, f32[3,2048]{1,0:T(4,128)} %pts_hbm.1, f32[64,2048]{1,0:T(8,128)} %basis_hbm.1, f32[8,64,64]{2,1,0:T(8,128)} %lt_hbm.1, f32[1,64,64]{2,1,0:T(8,128)} %ct_hbm.1, s32[8,12]{1,0:T(8,128)} %near_hbm.1, s32[1,4]{1,0:T(1,128)} %clist_ref.1, f32[1,4,64,64]{3,2,1,0:T(8,128)} %coup_hbm.1, ...), custom_call_target="tpu_custom_call" | custom-call | tf_op jit(solution)/shard_map/h2_product/pallas_call | solution.py:505
  31.6 1.7 %copy.11 = f32[32,2048]{1,0:T(8,128)} copy(f32[32,2048]{1,0:T(8,128)} %h2_product.1) | data formatting | bytes 524288
